TPU v7x, 512 devices: a whole 4x4x16 slice. The times are simulated.
512 devices in a mesh: gx: 32 (over z, x_lo), gy: 16 (over y, x_hi, core).
Axes of the slice: x: 4 (x_hi: 2, x_lo: 2; x = x_hi * 2 + x_lo), y: 4, z: 16, core: 2. Of those that a mesh axis runs over, the one named last changes fastest.
Arguments:
- field: float32 [256, 128, 192], P('gx', 'gy'), may hold values from -6 to 6
- target: float32 [256, 128, 192], P('gx', 'gy'), may hold values from -6 to 6
- embed_weight: float32 [192, 256], replicated, may hold values from -0.4375 to 0.4375
- norm_gain: float32 [256], replicated, may hold values from 0.5 to 1.5
- attend_weight: float32 [256, 768], replicated, may hold values from -0.375 to 0.375
- output_weight: float32 [256, 256], replicated, may hold values from -0.375 to 0.375
- second_gain: float32 [256], replicated, may hold values from 0.5 to 1.5
- expand_weight: float32 [256, 512], replicated, may hold values from -0.375 to 0.375
- reduce_weight: float32 [512, 256], replicated, may hold values from -0.25 to 0.25
- decode_weight: float32 [256, 192], replicated, may hold values from -0.375 to 0.375
Outputs:
- loss: float32 [], replicated
- field_gradient: float32 [256, 128, 192], P('gx', 'gy')
- embed_gradient: float32 [192, 256], replicated
- norm_gradient: float32 [256], replicated
- attend_gradient: float32 [256, 768], replicated
- output_gradient: float32 [256, 256], replicated
- second_gradient: float32 [256], replicated
- expand_gradient: float32 [256, 512], replicated
- reduce_gradient: float32 [512, 256], replicated
- decode_gradient: float32 [256, 192], replicated
All inputs are finite; a program needn't handle non-finite values.
Results may differ from a plain program's by a relative error of at most 0.0001.
Values sent between devices are 32-bit elements; how exact they have to be, the bound alone decides.
No kernel may reach another device: no remote copies, remote signals or barrier semaphores. Data moves between devices by JAX's collectives and lax.ppermute only.
A program may use at most 128 MiB of HBM per device.

v0:
```python
import jax
import jax.numpy as jnp
from jax import lax
from jax.sharding import PartitionSpec as P

PATCH = 4
HEADS = 8
STEPS = 2
EXACT = lax.Precision.HIGHEST
EPSILON = 1e-06
TIME_STEP = 0.1
VISCOSITY = 0.5


def with_halo(x, sides, width):
    for axis, dim in sides:
        count, length = (lax.axis_size(axis), x.shape[dim])
        up = [(i, (i + 1) % count) for i in range(count)]
        down = [(j, i) for i, j in up]
        last = lax.slice_in_dim(x, length - width, length, axis=dim)
        leading = lax.slice_in_dim(x, 0, width, axis=dim)
        before = lax.ppermute(last, axis, up)
        after = lax.ppermute(leading, axis, down)
        x = jnp.concatenate([before, x, after], axis=dim)
    return x


def matmul(left, right):
    return jnp.dot(left, right, precision=EXACT)


def rms_scale(values, gain):
    power = jnp.mean(values * values, axis=-1, keepdims=True)
    return values * lax.rsqrt(power + EPSILON) * gain


def closure(ext, params):
    (
        embed_weight,
        norm_gain,
        attend_weight,
        output_weight,
        second_gain,
        expand_weight,
        reduce_weight,
        decode_weight,
    ) = params
    wide, tall, depth = ext.shape
    levels = depth // 3
    across, along, upward = (wide // PATCH, tall // PATCH, levels // PATCH)
    patches = ext.reshape(across, PATCH, along, PATCH, 3, upward, PATCH).transpose(
        0, 2, 5, 4, 1, 3, 6
    )
    patches = patches.reshape(across, along, upward, 3 * PATCH * PATCH * PATCH)
    tokens = matmul(patches, embed_weight)
    width = tokens.shape[-1]
    head_size = width // HEADS
    mixed = matmul(rms_scale(tokens, norm_gain), attend_weight)
    inner_x, inner_y = (across - 2, along - 2)
    queries = mixed[1:-1, 1:-1, :, :width].reshape(inner_x, inner_y, upward, HEADS, head_size)
    keyset = mixed[:, :, :, width : 2 * width]
    valset = mixed[:, :, :, 2 * width :]
    offsets = [(shift_x, shift_y) for shift_x in range(3) for shift_y in range(3)]
    keyblock = jnp.concatenate(
        [keyset[sx : sx + inner_x, sy : sy + inner_y] for sx, sy in offsets], axis=2
    )
    valblock = jnp.concatenate(
        [valset[sx : sx + inner_x, sy : sy + inner_y] for sx, sy in offsets], axis=2
    )
    keyblock = keyblock.reshape(inner_x, inner_y, 9 * upward, HEADS, head_size)
    valblock = valblock.reshape(inner_x, inner_y, 9 * upward, HEADS, head_size)
    factor = head_size ** (-0.5)
    scores = jnp.einsum("xyzhe,xywhe->xyhzw", queries, keyblock, precision=EXACT) * factor
    weights = jnp.exp(scores)
    weights = weights / jnp.sum(weights, axis=-1, keepdims=True)
    attended = jnp.einsum("xyhzw,xywhe->xyzhe", weights, valblock, precision=EXACT)
    attended = attended.reshape(inner_x, inner_y, upward, width)
    middle = tokens[1:-1, 1:-1] + matmul(attended, output_weight)
    hidden = jax.nn.silu(matmul(rms_scale(middle, second_gain), expand_weight))
    middle = middle + matmul(hidden, reduce_weight)
    result = matmul(middle, decode_weight).reshape(inner_x, inner_y, upward, 3, PATCH, PATCH, PATCH)
    return result.transpose(0, 4, 1, 5, 3, 2, 6).reshape(inner_x * PATCH, inner_y * PATCH, depth)


def advance(ext, params):
    wide, tall, depth = ext.shape
    levels = depth // 3
    inner = ext[PATCH : wide - PATCH, PATCH : tall - PATCH]
    east = ext[PATCH + 1 : wide - PATCH + 1, PATCH : tall - PATCH]
    west = ext[PATCH - 1 : wide - PATCH - 1, PATCH : tall - PATCH]
    north = ext[PATCH : wide - PATCH, PATCH + 1 : tall - PATCH + 1]
    south = ext[PATCH : wide - PATCH, PATCH - 1 : tall - PATCH - 1]
    level = jnp.arange(depth, dtype=jnp.int32) % levels
    blank = jnp.zeros(inner.shape[:2] + (1,), jnp.float32)
    upper = jnp.where(level == levels - 1, 0.0, jnp.concatenate([inner[:, :, 1:], blank], axis=2))
    lower = jnp.where(level == 0, 0.0, jnp.concatenate([blank, inner[:, :, :-1]], axis=2))
    laplace = east + west + north + south + upper + lower - 6.0 * inner
    speed_x = jnp.concatenate([inner[:, :, 0:levels]] * 3, axis=2)
    speed_y = jnp.concatenate([inner[:, :, levels : 2 * levels]] * 3, axis=2)
    speed_z = jnp.concatenate([inner[:, :, 2 * levels :]] * 3, axis=2)
    carried = 0.5 * (
        speed_x * (east - west) + speed_y * (north - south) + speed_z * (upper - lower)
    )
    return inner + TIME_STEP * (VISCOSITY * laplace - carried + closure(ext, params))


def fold(spread, margin):
    for axis_dim in (0, 1):
        length = spread.shape[axis_dim] - 4 * margin
        middle = lax.slice_in_dim(spread, 2 * margin, 2 * margin + length, axis=axis_dim)
        lowside = lax.slice_in_dim(spread, 0, margin, axis=axis_dim)
        highside = lax.slice_in_dim(spread, length + 3 * margin, length + 4 * margin, axis=axis_dim)
        pad_low = [(0, 0), (0, 0), (0, 0)]
        pad_high = [(0, 0), (0, 0), (0, 0)]
        pad_low[axis_dim] = (0, length - margin)
        pad_high[axis_dim] = (length - margin, 0)
        spread = middle + jnp.pad(lowside, pad_low) + jnp.pad(highside, pad_high)
    return spread


def shards(
    field,
    target,
    embed_weight,
    norm_gain,
    attend_weight,
    output_weight,
    second_gain,
    expand_weight,
    reduce_weight,
    decode_weight,
):
    params = (
        embed_weight,
        norm_gain,
        attend_weight,
        output_weight,
        second_gain,
        expand_weight,
        reduce_weight,
        decode_weight,
    )
    energy = lax.psum(jnp.sum(target * target), ("gx", "gy"))
    current = field
    pullbacks = []
    for step in range(STEPS):
        extended = with_halo(current, (("gx", 0), ("gy", 1)), PATCH)
        current, pullback = jax.vjp(advance, extended, params)
        pullbacks.append(pullback)
    residue = current - target
    cotangent = 2.0 * residue
    gradients = None
    for pullback in reversed(pullbacks):
        back_ext, back_params = pullback(cotangent)
        gradients = (
            back_params if gradients is None else jax.tree.map(jnp.add, gradients, back_params)
        )
        spread = with_halo(back_ext, (("gx", 0), ("gy", 1)), PATCH)
        cotangent = fold(spread, PATCH)
    local_misfit = jnp.sum(residue * residue)
    misfit = lax.psum(local_misfit, ("gx", "gy"))
    summed = lax.psum(tuple(gradients), ("gx", "gy"))
    entries = (
        field.shape[0] * lax.axis_size("gx") * field.shape[1] * lax.axis_size("gy") * field.shape[2]
    )
    scale = jnp.float32(entries) / energy
    loss = misfit / energy
    return (loss, scale * cotangent) + tuple((scale * piece for piece in summed))


def solution(mesh):
    in_specs = (P("gx", "gy", None), P("gx", "gy", None), P(), P(), P(), P(), P(), P(), P(), P())
    out_specs = (P(), P("gx", "gy", None), P(), P(), P(), P(), P(), P(), P(), P())
    return jax.shard_map(shards, mesh=mesh, in_specs=in_specs, out_specs=out_specs, check_vma=False)
```

profile of v0, /device:TPU:1, one launch (start us, length us, event | category | flops | bytes accessed | tf_op | source)
XLA Modules:
  0.0 810.8 jit_solution(4378260794345569212)
XLA Ops:
  8.1 12.9 %collective-permute-start = (f32[4,8,192]{2,1,0:T(8,128)S(1)}, f32[4,8,192]{2,1,0:T(8,128)S(1)}, u32[]{:S(2)}, u32[]{:S(2)}) collective-permute-start(f32[4,8,192]{2,1,0:T(8,128)S(1)} %get-tuple-element.154), channel_id=1, source_target_pairs={{16,0},{32,16},{48,32},{64,48},{80,64},{96,80},{112,96},{128,112},... | collective-permute-start | bytes 73736 | tf_op jit(solution)/shard_map/ppermute | solution.py:23
  29.2 6.3 collective-permute-start.3
  38.2 4.5 collective-permute-done.2
  43.3 5.0 reshape.216
  48.4 6.5 copy.78
  74.2 5.5 collective-permute-start.4
  86.4 4.5 collective-permute-done.6
  90.9 5.0 reshape.224
  96.0 7.0 copy.86
  103.0 3.9 multiply_reduce_fusion.6
  154.1 3.2 fusion.169
  191.8 6.1 copy.118
  198.1 5.1 reshape.239
  205.6 5.6 collective-permute-start.9
  212.6 3.2 collective-permute-start.10
  215.8 4.0 collective-permute-start.11
  262.6 3.3 fusion.168
  293.5 6.3 copy.143
  299.8 5.0 reshape.247
  307.9 5.5 collective-permute-start.13
  313.4 107.6 %all-reduce.72 = (f32[]{:T(128)}, f32[]{:T(128)}, f32[256]{0:T(256)S(1)}, f32[256]{0:T(256)S(1)}) all-reduce(f32[]{:T(128)} %get-tuple-element.141, f32[]{:T(128)} %multiply_reduce_fusion.12, f32[256]{0:T(256)S(1)} %add.385, f32[256]{0:T(256)S(1)} %add.388), channel_id=1, replica_groups=mesh['gx'=32,'gy'=16] {'gx','gy'}, use_global_device_ids=true, to_apply=%region_7.8 | all-reduce | flops 514 | bytes 4112 | tf_op jit(solution)/shard_map/psum | solution.py:161
  422.3 3.5 collective-permute-start.14
  429.7 3.6 collective-permute-done.15
  434.2 360.8 %all-reduce.76.cloned.1.call-done = (f32[192,256]{1,0:T(8,128)}, f32[256,768]{1,0:T(8,128)}, f32[256,256]{1,0:T(8,128)}, f32[256,512]{1,0:T(8,128)}, f32[512,256]{1,0:T(8,128)}, /*index=5*/f32[256,192]{0,1:T(8,128)}) async-done(((f32[192,256]{1,0:T(8,128)}, f32[256,768]{1,0:T(8,128)}, f32[256,256]{1,0:T(8,128)}, f32[256,512]{1,0:T(8,128)}, f32[512,256]{1,0:T(8,128)}, /*index=5*/f32[256,192]{0,1:T(8,128)}), ...) | async-done | bytes 2490384 | tf_op jit(solution)/shard_map/psum | solution.py:162
  (632 shorter events, 206.8 us)
Async XLA Ops:
  7.2 51.0 %copy-start = (f32[256,768]{1,0:T(8,128)S(1)}, f32[256,768]{1,0:T(8,128)}, u32[]{:S(2)}) copy-start(f32[256,768]{1,0:T(8,128)} %param.14) | copy-start | bytes 2359300
  7.2 787.8 %all-reduce.76.cloned.1.call-start = ((), (), s32[]{:S(2)}) async-start(), calls=%async_computation | async-start | bytes 4980736 | tf_op jit(solution)/shard_map/psum | solution.py:162
  8.1 20.5 %collective-permute-start = (f32[4,8,192]{2,1,0:T(8,128)S(1)}, f32[4,8,192]{2,1,0:T(8,128)S(1)}, u32[]{:S(2)}, u32[]{:S(2)}) collective-permute-start(f32[4,8,192]{2,1,0:T(8,128)S(1)} %get-tuple-element.154), channel_id=1, source_target_pairs={{16,0},{32,16},{48,32},{64,48},{80,64},{96,80},{112,96},{128,112},... | collective-permute-start | bytes 73736 | tf_op jit(solution)/shard_map/ppermute | solution.py:23
  20.9 6.8 collective-permute-start.1
  29.2 9.0 %collective-permute-start.3 = (f32[16,4,192]{2,1,0:T(4,128)S(1)}, f32[16,4,192]{2,1,0:T(4,128)S(1)}, u32[]{:S(2)}, u32[]{:S(2)}) collective-permute-start(f32[16,4,192]{2,1,0:T(4,128)S(1)} %get-tuple-element.122), channel_id=1, source_target_pairs={{0,1},{1,2},{2,3},{3,4},{4,5},{5,6},{6,7},{7,8},{8,9},{9,10},{10,1... | collective-permute-start | bytes 147464 | tf_op jit(solution)/shard_map/ppermute | solution.py:22
  35.5 7.1 collective-permute-start.2
  37.5 33.5 %copy-start.191 = (pred[192]{0:T(512)(128)(4,1)}, pred[192]{0:T(512)(128)(4,1)S(1)}, u32[]{:S(2)}) copy-start(pred[192]{0:T(512)(128)(4,1)S(1)} %get-tuple-element.177) | copy-start | bytes 580
  37.5 33.5 %copy-start.196 = (pred[192]{0:T(512)(128)(4,1)}, pred[192]{0:T(512)(128)(4,1)S(1)}, u32[]{:S(2)}) copy-start(pred[192]{0:T(512)(128)(4,1)S(1)} %get-tuple-element.176) | copy-start | bytes 580
  72.3 8.1 %collective-permute-start.5 = (f32[4,8,192]{2,1,0:T(8,128)S(1)}, f32[4,8,192]{2,1,0:T(8,128)S(1)}, u32[]{:S(2)}, u32[]{:S(2)}) collective-permute-start(f32[4,8,192]{2,1,0:T(8,128)S(1)} %get-tuple-element.147), channel_id=1, source_target_pairs={{0,16},{16,32},{32,48},{48,64},{64,80},{80,96},{96,112},{112,128},... | collective-permute-start | bytes 73736 | tf_op jit(solution)/shard_map/ppermute | solution.py:22
  74.2 6.5 collective-permute-start.4
  80.7 5.6 collective-permute-start.7
  83.7 7.1 collective-permute-start.6
  203.2 16.6 %copy-start.155 = (f32[2,2,8,16]{3,2,1,0:T(8,128)S(1)}, f32[2,2,8,16]{3,2,1,0:T(8,128)}, u32[]{:S(2)}) copy-start(f32[2,2,8,16]{3,2,1,0:T(8,128)} %copy-done.154) | copy-start | bytes 6148
  203.5 20.1 %copy-start.194 = (pred[8]{0:T(512)(128)(4,1)S(1)}, pred[8]{0:T(512)(128)(4,1)}, u32[]{:S(2)}) copy-start(pred[8]{0:T(512)(128)(4,1)} %constant.73.clone.1) | copy-start | bytes 28
  203.7 20.0 %copy-start.108 = (f32[8,8,64]{2,1,0:T(8,128)S(1)}, f32[8,8,64]{2,1,0:T(8,128)}, u32[]{:S(2)}) copy-start(f32[8,8,64]{2,1,0:T(8,128)} %get-tuple-element.152) | copy-start | bytes 49156
  203.7 8.3 %collective-permute-start.8 = (f32[4,16,192]{2,1,0:T(8,128)S(1)}, f32[4,16,192]{2,1,0:T(8,128)S(1)}, u32[]{:S(2)}, u32[]{:S(2)}) collective-permute-start(f32[4,16,192]{2,1,0:T(8,128)S(1)} %get-tuple-element.112), channel_id=1, source_target_pairs={{0,16},{16,32},{32,48},{48,64},{64,80},{80,96},{96,112},{112,128},... | collective-permute-start | bytes 147464 | tf_op jit(solution)/shard_map/ppermute | solution.py:22
  205.6 6.9 collective-permute-start.9
  212.6 7.8 collective-permute-start.10
  215.8 7.7 collective-permute-start.11
  305.2 128.2 %copy-start.195 = (pred[8]{0:T(512)(128)(4,1)S(1)}, pred[8]{0:T(512)(128)(4,1)}, u32[]{:S(2)}) copy-start(pred[8]{0:T(512)(128)(4,1)} %constant.73.clone.1) | copy-start | bytes 28
  306.0 116.3 %collective-permute-start.12 = (f32[4,16,192]{2,1,0:T(8,128)S(1)}, f32[4,16,192]{2,1,0:T(8,128)S(1)}, u32[]{:S(2)}, u32[]{:S(2)}) collective-permute-start(f32[4,16,192]{2,1,0:T(8,128)S(1)} %get-tuple-element.110), channel_id=1, source_target_pairs={{0,16},{16,32},{32,48},{48,64},{64,80},{80,96},{96,112},{112,128},... | collective-permute-start | bytes 147464 | tf_op jit(solution)/shard_map/ppermute | solution.py:22
  307.9 114.4 %collective-permute-start.13 = (f32[4,16,192]{2,1,0:T(8,128)S(1)}, f32[4,16,192]{2,1,0:T(8,128)S(1)}, u32[]{:S(2)}, u32[]{:S(2)}) collective-permute-start(f32[4,16,192]{2,1,0:T(8,128)S(1)} %get-tuple-element.111), channel_id=1, source_target_pairs={{16,0},{32,16},{48,32},{64,48},{80,64},{96,80},{112,96},{128,112},... | collective-permute-start | bytes 147464 | tf_op jit(solution)/shard_map/ppermute | solution.py:23
  422.3 7.4 collective-permute-start.14
  425.9 7.4 collective-permute-start.15
  (197 other events, 830.2 us)
Sparse Core Ops, SparseCore 0:
  305.3 489.6 all-reduce.75
where the time goes:
time: 823 us; the launch traced here: 811 us
  waiting for transfers between devices  379 us (46%)
  local copies, waits for them, and re-layouts  147 us (18%)
  blocking collectives  108 us (13%)
  matrix products  67.6 us (8%)
  starting transfers between devices  63 us (8%)
  other arithmetic  26.2 us (3%)
  between operations  20.3 us (2%)
    psum x1, waiting for transfers between devices, shards(): summed = lax.psum(tuple(gradients), ('gx', 'gy'))  361 us
    psum x1, blocking collectives, shards(): misfit = lax.psum(local_misfit, ('gx', 'gy'))  108 us
    unnamed x462, local copies, waits for them, and re-layouts  58.7 us
    dot_general x36, matrix products, matmul(): return jnp.dot(left, right, precision=EXACT)  49.2 us
    ppermute x8, starting transfers between devices, with_halo(): after = lax.ppermute(leading, axis, down)  39.2 us
    transpose x4, local copies, waits for them, and re-layouts, closure(): ext.reshape(across, PATCH, along, PATCH, 3, upward, PATCH)  25.9 us
    ppermute x8, starting transfers between devices, with_halo(): before = lax.ppermute(last, axis, up)  23.7 us
    reshape x4, local copies, waits for them, and re-layouts, closure(): ext.reshape(across, PATCH, along, PATCH, 3, upward, PATCH)  20.2 us
  transfers between devices with their start and end apart: 17, of which 8 were waited for; matrix products, arithmetic and copies ran while one was open for 1% of the time, Pallas kernels for 0%

commit v1 on v0

--- a/solution.py
+++ b/solution.py
@@ -10,6 +10,11 @@
 EPSILON = 1e-06
 TIME_STEP = 0.1
 VISCOSITY = 0.5
+
+
+def map_pipes_on(content, axis_id, axis_key):
+    local_part = lax.psum(content, axis_id)
+    return lax.psum(local_part, axis_key)
 
 
 def with_halo(x, sides, width):
@@ -159,7 +164,7 @@
         cotangent = fold(spread, PATCH)
     local_misfit = jnp.sum(residue * residue)
     misfit = lax.psum(local_misfit, ("gx", "gy"))
-    summed = lax.psum(tuple(gradients), ("gx", "gy"))
+    summed = map_pipes_on(tuple(gradients), "gx", "gy")
     entries = (
         field.shape[0] * lax.axis_size("gx") * field.shape[1] * lax.axis_size("gy") * field.shape[2]
     )

time: 823 us -> 759 us (0.922)
  waiting for transfers between devices: 379 us -> 196 us
  blocking collectives: 108 us -> 222 us
    psum x1 -> x2, waiting for transfers between devices: 361 us -> 183 us  [the longest x1 132 us: map_pipes_on(): local_part = lax.psum(content, axis_id)]
    psum x0 -> x2, blocking collectives: none -> 119 us  [the longest x1 67.6 us: map_pipes_on(): return lax.psum(local_part, axis_key)]
    ppermute x8, waiting for transfers between devices: 16.4 us -> 2.41 us  [with_halo(): after = lax.ppermute(leading, axis, down)]
    ppermute x8, waiting for transfers between devices: 1.71 us -> 10.7 us  [with_halo(): before = lax.ppermute(last, axis, up)]
  transfers between devices with their start and end apart: 17 -> 18, of which waited for: 8 -> 8; matrix products, arithmetic and copies ran while one was open for 1% -> 3% of each run, Pallas kernels for 0% -> 0%
where the time goes in v1:
time: 759 us; the launch traced here: 746 us
  blocking collectives  222 us (29%)
  waiting for transfers between devices  196 us (26%)
  local copies, waits for them, and re-layouts  147 us (19%)
  starting transfers between devices  68.2 us (9%)
  matrix products  65.8 us (9%)
  other arithmetic  27 us (4%)
  between operations  20.4 us (3%)
    psum x1, waiting for transfers between devices, map_pipes_on(): local_part = lax.psum(content, axis_id)  132 us
    psum x1, blocking collectives, shards(): misfit = lax.psum(local_misfit, ('gx', 'gy'))  104 us
    psum x1, blocking collectives, map_pipes_on(): return lax.psum(local_part, axis_key)  67.6 us
    unnamed x462, local copies, waits for them, and re-layouts  60.1 us
    psum x1, blocking collectives, map_pipes_on(): local_part = lax.psum(content, axis_id)  51 us
    psum x1, waiting for transfers between devices, map_pipes_on(): return lax.psum(local_part, axis_key)  50.3 us
    dot_general x36, matrix products, matmul(): return jnp.dot(left, right, precision=EXACT)  48.3 us
    ppermute x8, starting transfers between devices, with_halo(): after = lax.ppermute(leading, axis, down)  43 us
  transfers between devices with their start and end apart: 18, of which 8 were waited for; matrix products, arithmetic and copies ran while one was open for 3% of the time, Pallas kernels for 0%

profile of v1, /device:TPU:1, one launch (start us, length us, event | category | flops | bytes accessed | tf_op | source)
XLA Modules:
  0.0 746.4 jit_solution(10070879635020597356)
XLA Ops:
  8.1 3.9 collective-permute-start.1
  12.0 10.9 %collective-permute-start = (f32[4,8,192]{2,1,0:T(8,128)S(1)}, f32[4,8,192]{2,1,0:T(8,128)S(1)}, u32[]{:S(2)}, u32[]{:S(2)}) collective-permute-start(f32[4,8,192]{2,1,0:T(8,128)S(1)} %get-tuple-element.162), channel_id=1, source_target_pairs={{16,0},{32,16},{48,32},{64,48},{80,64},{96,80},{112,96},{128,112},... | collective-permute-start | bytes 73736 | tf_op jit(solution)/shard_map/ppermute | solution.py:28
  30.4 4.3 collective-permute-start.3
  38.0 5.1 reshape.216
  43.1 6.5 copy.78
  75.2 3.5 collective-permute-done.5
  78.8 9.9 %collective-permute-start.6 = (f32[16,4,192]{2,1,0:T(4,128)S(1)}, f32[16,4,192]{2,1,0:T(4,128)S(1)}, u32[]{:S(2)}, u32[]{:S(2)}) collective-permute-start(f32[16,4,192]{2,1,0:T(4,128)S(1)} %get-tuple-element.129), channel_id=1, source_target_pairs={{1,0},{2,1},{3,2},{4,3},{5,4},{6,5},{7,6},{8,7},{9,8},{10,9},{11,1... | collective-permute-start | bytes 147464 | tf_op jit(solution)/shard_map/ppermute | solution.py:28
  92.0 5.1 reshape.224
  97.1 7.0 copy.86
  104.1 3.9 multiply_reduce_fusion.6
  153.1 3.2 fusion.170
  191.6 6.3 copy.118
  198.0 5.1 reshape.239
  205.6 3.5 collective-permute-start.8
  209.1 3.7 collective-permute-done.8
  212.9 9.2 %collective-permute-start.11 = (f32[24,4,192]{2,1,0:T(4,128)S(1)}, f32[24,4,192]{2,1,0:T(4,128)S(1)}, u32[]{:S(2)}, u32[]{:S(2)}) collective-permute-start(f32[24,4,192]{2,1,0:T(4,128)S(1)} %get-tuple-element.117), channel_id=1, source_target_pairs={{1,0},{2,1},{3,2},{4,3},{5,4},{6,5},{7,6},{8,7},{9,8},{10,9},{11,1... | collective-permute-start | bytes 221192 | tf_op jit(solution)/shard_map/ppermute | solution.py:28
  293.6 103.6 %all-reduce.72 = (f32[]{:T(128)}, f32[]{:T(128)}) all-reduce(f32[]{:T(128)} %get-tuple-element.149, f32[]{:T(128)} %multiply_reduce_fusion.12), channel_id=1, replica_groups=mesh['gx'=32,'gy'=16] {'gx','gy'}, use_global_device_ids=true, to_apply=%region_7.8 | all-reduce | flops 2 | bytes 16 | tf_op jit(solution)/shard_map/psum | solution.py:166
  400.8 6.3 copy.143
  407.0 5.0 reshape.247
  412.2 132.2 %all-reduce.80.cloned.1.call-done = (f32[192,256]{1,0:T(8,128)}, f32[256,768]{1,0:T(8,128)}, f32[256,256]{1,0:T(8,128)}, f32[256,512]{1,0:T(8,128)}, f32[512,256]{1,0:T(8,128)}, /*index=5*/f32[256,192]{0,1:T(8,128)}) async-done(((f32[192,256]{1,0:T(8,128)}, f32[256,768]{1,0:T(8,128)}, f32[256,256]{1,0:T(8,128)}, f32[256,512]{1,0:T(8,128)}, f32[512,256]{1,0:T(8,128)}, /*index=5*/f32[256,192]{0,1:T(8,128)}), ...) | async-done | bytes 2490384 | tf_op jit(solution)/shard_map/psum | solution.py:16
  550.9 51.0 %all-reduce.73 = (f32[256]{0:T(256)S(1)}, f32[256]{0:T(256)S(1)}) all-reduce(f32[256]{0:T(256)S(1)} %add.401, f32[256]{0:T(256)S(1)} %add.404), channel_id=1, replica_groups=mesh['gx'=32,'gy'=16] {'gx'}, use_global_device_ids=true, to_apply=%region_20.21 | all-reduce | flops 512 | bytes 4096 | tf_op jit(solution)/shard_map/psum | solution.py:16
  601.9 67.6 %all-reduce.75 = (f32[256]{0:T(256)S(1)}, f32[256]{0:T(256)S(1)}) all-reduce(f32[256]{0:T(256)S(1)} %get-tuple-element.20, f32[256]{0:T(256)S(1)} %get-tuple-element.21), channel_id=1, replica_groups=mesh['gx'=32,'gy'=16] {'gy'}, use_global_device_ids=true, to_apply=%region_21.22 | all-reduce | flops 512 | bytes 4096 | tf_op jit(solution)/shard_map/psum | solution.py:17
  672.7 4.5 collective-permute-start.14
  681.1 50.3 %all-reduce.82.cloned.1.call-done = (f32[192,256]{1,0:T(8,128)}, f32[256,768]{1,0:T(8,128)}, f32[256,256]{1,0:T(8,128)}, f32[256,512]{1,0:T(8,128)}, f32[512,256]{1,0:T(8,128)}, /*index=5*/f32[256,192]{0,1:T(8,128)}) async-done(((f32[192,256]{1,0:T(8,128)}, f32[256,768]{1,0:T(8,128)}, f32[256,256]{1,0:T(8,128)}, f32[256,512]{1,0:T(8,128)}, f32[512,256]{1,0:T(8,128)}, /*index=5*/f32[256,192]{0,1:T(8,128)}), ...) | async-done | bytes 2490384 | tf_op jit(solution)/shard_map/psum | solution.py:17
  (637 shorter events, 214.5 us)
Async XLA Ops:
  7.2 537.2 %all-reduce.80.cloned.1.call-start = ((), (), s32[]{:S(2)}) async-start(), calls=%async_computation | async-start | bytes 4980736 | tf_op jit(solution)/shard_map/psum | solution.py:16
  8.1 17.9 %collective-permute-start.1 = (f32[4,8,192]{2,1,0:T(8,128)S(1)}, f32[4,8,192]{2,1,0:T(8,128)S(1)}, u32[]{:S(2)}, u32[]{:S(2)}) collective-permute-start(f32[4,8,192]{2,1,0:T(8,128)S(1)} %get-tuple-element.163), channel_id=1, source_target_pairs={{0,16},{16,32},{32,48},{48,64},{64,80},{80,96},{96,112},{112,128},... | collective-permute-start | bytes 73736 | tf_op jit(solution)/shard_map/ppermute | solution.py:27
  12.0 14.9 %collective-permute-start = (f32[4,8,192]{2,1,0:T(8,128)S(1)}, f32[4,8,192]{2,1,0:T(8,128)S(1)}, u32[]{:S(2)}, u32[]{:S(2)}) collective-permute-start(f32[4,8,192]{2,1,0:T(8,128)S(1)} %get-tuple-element.162), channel_id=1, source_target_pairs={{16,0},{32,16},{48,32},{64,48},{80,64},{96,80},{112,96},{128,112},... | collective-permute-start | bytes 73736 | tf_op jit(solution)/shard_map/ppermute | solution.py:28
  27.5 7.8 %collective-permute-start.2 = (f32[16,4,192]{2,1,0:T(4,128)S(1)}, f32[16,4,192]{2,1,0:T(4,128)S(1)}, u32[]{:S(2)}, u32[]{:S(2)}) collective-permute-start(f32[16,4,192]{2,1,0:T(4,128)S(1)} %get-tuple-element.131), channel_id=1, source_target_pairs={{1,0},{2,1},{3,2},{4,3},{5,4},{6,5},{7,6},{8,7},{9,8},{10,9},{11,1... | collective-permute-start | bytes 147464 | tf_op jit(solution)/shard_map/ppermute | solution.py:28
  30.4 7.0 collective-permute-start.3
  69.2 6.0 collective-permute-start.4
  72.0 6.8 collective-permute-start.5
  78.8 12.5 %collective-permute-start.6 = (f32[16,4,192]{2,1,0:T(4,128)S(1)}, f32[16,4,192]{2,1,0:T(4,128)S(1)}, u32[]{:S(2)}, u32[]{:S(2)}) collective-permute-start(f32[16,4,192]{2,1,0:T(4,128)S(1)} %get-tuple-element.129), channel_id=1, source_target_pairs={{1,0},{2,1},{3,2},{4,3},{5,4},{6,5},{7,6},{8,7},{9,8},{10,9},{11,1... | collective-permute-start | bytes 147464 | tf_op jit(solution)/shard_map/ppermute | solution.py:28
  88.7 3.2 collective-permute-start.7
  203.6 5.5 collective-permute-start.9
  205.6 7.3 collective-permute-start.8
  212.9 12.0 %collective-permute-start.11 = (f32[24,4,192]{2,1,0:T(4,128)S(1)}, f32[24,4,192]{2,1,0:T(4,128)S(1)}, u32[]{:S(2)}, u32[]{:S(2)}) collective-permute-start(f32[24,4,192]{2,1,0:T(4,128)S(1)} %get-tuple-element.117), channel_id=1, source_target_pairs={{1,0},{2,1},{3,2},{4,3},{5,4},{6,5},{7,6},{8,7},{9,8},{10,9},{11,1... | collective-permute-start | bytes 221192 | tf_op jit(solution)/shard_map/ppermute | solution.py:28
  222.1 3.5 collective-permute-start.10
  292.9 438.4 %all-reduce.82.cloned.1.call-start = ((), (), s32[]{:S(2)}) async-start(), calls=%async_computation.1 | async-start | bytes 4980736 | tf_op jit(solution)/shard_map/psum | solution.py:17
  412.0 132.5 %copy-start.109 = (f32[8,8,192]{2,1,0:T(8,128)S(1)}, f32[8,8,192]{2,1,0:T(8,128)}, u32[]{:S(2)}) copy-start(f32[8,8,192]{2,1,0:T(8,128)} %get-tuple-element.139) | copy-start | bytes 147460
  412.0 132.6 %copy-start.82 = (f32[8,8,192]{2,1,0:T(8,128)S(1)}, f32[8,8,192]{2,1,0:T(8,128)}, u32[]{:S(2)}) copy-start(f32[8,8,192]{2,1,0:T(8,128)} %get-tuple-element.140) | copy-start | bytes 147460
  412.0 132.6 %copy-start.83 = (f32[8,8,192]{2,1,0:T(8,128)S(1)}, f32[8,8,192]{2,1,0:T(8,128)}, u32[]{:S(2)}) copy-start(f32[8,8,192]{2,1,0:T(8,128)} %get-tuple-element.142) | copy-start | bytes 147460
  412.1 132.6 %copy-start.193 = (pred[192]{0:T(512)(128)(4,1)S(1)}, pred[192]{0:T(512)(128)(4,1)}, u32[]{:S(2)}) copy-start(pred[192]{0:T(512)(128)(4,1)} %copy-done.191) | copy-start | bytes 580
  412.1 132.6 %copy-start.203 = (pred[191]{0:T(512)(128)(4,1)S(1)}, pred[191]{0:T(512)(128)(4,1)}, u32[]{:S(2)}) copy-start(pred[191]{0:T(512)(128)(4,1)} %slice.447) | copy-start | bytes 577
  545.4 134.9 %copy-start.195 = (pred[8]{0:T(512)(128)(4,1)S(1)}, pred[8]{0:T(512)(128)(4,1)}, u32[]{:S(2)}) copy-start(pred[8]{0:T(512)(128)(4,1)} %constant.73.clone.1) | copy-start | bytes 28
  545.5 124.6 %collective-permute-start.13 = (f32[4,16,192]{2,1,0:T(8,128)S(1)}, f32[4,16,192]{2,1,0:T(8,128)S(1)}, u32[]{:S(2)}, u32[]{:S(2)}) collective-permute-start(f32[4,16,192]{2,1,0:T(8,128)S(1)} %get-tuple-element.119), channel_id=1, source_target_pairs={{16,0},{32,16},{48,32},{64,48},{80,64},{96,80},{112,96},{128,112},... | collective-permute-start | bytes 147464 | tf_op jit(solution)/shard_map/ppermute | solution.py:28
  548.4 121.7 %collective-permute-start.12 = (f32[4,16,192]{2,1,0:T(8,128)S(1)}, f32[4,16,192]{2,1,0:T(8,128)S(1)}, u32[]{:S(2)}, u32[]{:S(2)}) collective-permute-start(f32[4,16,192]{2,1,0:T(8,128)S(1)} %get-tuple-element.118), channel_id=1, source_target_pairs={{0,16},{16,32},{32,48},{48,64},{64,80},{80,96},{96,112},{112,128},... | collective-permute-start | bytes 147464 | tf_op jit(solution)/shard_map/ppermute | solution.py:27
  670.1 10.0 %collective-permute-start.15 = (f32[24,4,192]{2,1,0:T(4,128)S(1)}, f32[24,4,192]{2,1,0:T(4,128)S(1)}, u32[]{:S(2)}, u32[]{:S(2)}) collective-permute-start(f32[24,4,192]{2,1,0:T(4,128)S(1)} %get-tuple-element.115), channel_id=1, source_target_pairs={{1,0},{2,1},{3,2},{4,3},{5,4},{6,5},{7,6},{8,7},{9,8},{10,9},{11,1... | collective-permute-start | bytes 221192 | tf_op jit(solution)/shard_map/ppermute | solution.py:28
  672.7 7.5 %collective-permute-start.14 = (f32[24,4,192]{2,1,0:T(4,128)S(1)}, f32[24,4,192]{2,1,0:T(4,128)S(1)}, u32[]{:S(2)}, u32[]{:S(2)}) collective-permute-start(f32[24,4,192]{2,1,0:T(4,128)S(1)} %get-tuple-element.114), channel_id=1, source_target_pairs={{0,1},{1,2},{2,3},{3,4},{4,5},{5,6},{6,7},{7,8},{8,9},{9,10},{10,1... | collective-permute-start | bytes 221192 | tf_op jit(solution)/shard_map/ppermute | solution.py:27
  (198 other events, 1339.4 us)
Sparse Core Ops, SparseCore 0:
  293.1 251.2 all-reduce.79
  547.8 183.5 all-reduce.81
